TPU v7x, 32 devices: a whole 2x2x4 slice. The times are simulated.
32 devices in a mesh: ep: 4 (over y, core), etp: 8 (over z, x).
Axes of the slice: x: 2, y: 2, z: 4, core: 2. Of those that a mesh axis runs over, the one named last changes fastest.
Arguments:
- tokens: bfloat16 [4096, 7168], P(('ep', 'etp')), may hold values from -6 to 6
- expert_ids: int32 [4096, 8], P(('ep', 'etp')), may hold values from 0 to 383, all different within a row; in each aligned block of 128 rows (0 to 127, 128 to 255, ...) at most 3 rows name the same one
- gate_q: int32 [4096, 8], P(('ep', 'etp')), may hold values from 1 to 1024
- w_gate: bfloat16 [4, 7168, 2048], P('ep', None, 'etp'), may hold values from -0.0625 to 0.0625
- w_up: bfloat16 [4, 7168, 2048], P('ep', None, 'etp'), may hold values from -0.0625 to 0.0625
- w_down: bfloat16 [4, 2048, 7168], P('ep', 'etp'), may hold values from -0.125 to 0.125
Outputs:
- mixed: bfloat16 [4096, 7168], P(('ep', 'etp'))
Inputs may be any that keep to these rules, and one draw needn't show every extreme that they name: `expert_ids`: each row names 8 different experts; among the 128 rows of one device no expert is named by more than 3 rows.
All inputs are finite; a program needn't handle non-finite values.
Results may differ from a plain program's by a relative error of at most 0.014.
Values may be sent and summed in bfloat16 or wider, within the bound.
A program may use at most 64 MiB of HBM per device.

v0:
```python
import jax
import jax.numpy as jnp
from jax import lax
from jax.sharding import PartitionSpec as P

CAP = 3


def body(tokens, expert_ids, gate_q, w_gate, w_up, w_down):
    groups = lax.axis_size("ep")
    members = lax.axis_size("etp")
    capacity = CAP
    width = tokens.shape[1]
    count_rows = tokens.shape[0]
    flat_ids = expert_ids.reshape(-1)
    owner_hot = (flat_ids[:, None] == jnp.arange(groups, dtype=jnp.int32)[None, :]).astype(
        jnp.int32
    )
    earlier = jnp.cumsum(owner_hot, axis=0) - owner_hot
    position = jnp.sum(earlier * owner_hot, axis=1)
    column = jnp.where(flat_ids < groups, flat_ids * capacity + position, -1)
    select = (column[:, None] == jnp.arange(groups * capacity, dtype=jnp.int32)[None, :]).astype(
        jnp.float32
    )
    select = select.reshape(count_rows, -1, groups * capacity)
    placing = jnp.sum(select, axis=1)
    gate_scale = gate_q.astype(jnp.float32) / 1024.0
    scaling = jnp.sum(select * gate_scale[:, :, None], axis=1)
    bucket = jnp.einsum(
        "tc,td->cd", placing.astype(jnp.bfloat16), tokens, preferred_element_type=jnp.float32
    )
    bucket = bucket.astype(jnp.bfloat16).reshape(groups, capacity, width)
    gathered = lax.all_gather(bucket, "etp", axis=1, tiled=True)
    arrived = lax.all_to_all(gathered, "ep", split_axis=0, concat_axis=0, tiled=True)
    gate = jnp.dot(arrived, w_gate[0], preferred_element_type=jnp.float32)
    upper = jnp.dot(arrived, w_up[0], preferred_element_type=jnp.float32)
    hidden = (jax.nn.silu(gate) * upper).astype(jnp.bfloat16)
    inner = hidden.shape[2]
    ordered = (
        hidden.reshape(groups, members, capacity, inner).transpose(1, 0, 2, 3).reshape(-1, inner)
    )
    term = jnp.dot(ordered, w_down[0], preferred_element_type=jnp.float32)
    rounded = lax.optimization_barrier(term.astype(jnp.bfloat16))
    summed = lax.psum_scatter(
        rounded.astype(jnp.float32).astype(jnp.bfloat16), "etp", scatter_dimension=0, tiled=True
    )
    local_out = summed.reshape(groups, capacity, width)
    results = lax.all_to_all(local_out, "ep", split_axis=0, concat_axis=0, tiled=True)
    flat_out = results.reshape(groups * capacity, width).astype(jnp.float32)
    mixed = jnp.dot(scaling, flat_out, precision=lax.Precision.HIGHEST)
    return mixed.astype(jnp.bfloat16)


def solution(mesh):
    in_specs = (
        P(("ep", "etp"), None),
        P(("ep", "etp"), None),
        P(("ep", "etp"), None),
        P("ep", None, "etp"),
        P("ep", None, "etp"),
        P("ep", "etp", None),
    )
    out_specs = P(("ep", "etp"), None)
    return jax.shard_map(body, mesh=mesh, in_specs=in_specs, out_specs=out_specs, check_vma=False)
```

profile of v0, /device:TPU:0, one launch (start us, length us, event | category | flops | bytes accessed | tf_op | source)
XLA Modules:
  0.0 157.0 jit_solution(10917868213449177721)
XLA Ops:
  6.5 0.9 copy.40
  7.5 0.1 eq.43
  7.6 0.1 eq.39
  7.7 1.1 reduce-window.6
  8.8 0.2 slice_reduce_fusion
  9.0 0.2 reduce-window.9
  9.2 0.1 add_bitcast_fusion
  9.3 0.1 reduce_sum.30
  9.4 0.7 add_select_fusion
  10.2 0.7 convert_multiply_fusion
  10.9 0.3 convolution_convert_fusion.2
  11.2 0.1 reshape.56
  11.4 0.8 copy.43
  12.2 45.0 %all-gather.2.cloned.1.call-done = bf16[4,24,7168]{2,0,1:T(4,128)(2,1)} async-done(((bf16[4,3,7168]{2,0,1:T(4,128)(2,1)}), bf16[4,24,7168]{2,0,1:T(4,128)(2,1)}) %all-gather.2.cloned.1.call-update) | async-done | bytes 1376272 | tf_op jit(solution)/shard_map/all_gather | solution.py:33
  57.2 1.9 %copy.44 = bf16[4,24,7168]{2,1,0:T(8,128)(2,1)S(1)} copy(bf16[4,24,7168]{2,0,1:T(4,128)(2,1)} %all-gather.2.cloned.1.call-done) | data formatting | bytes 2752512 | tf_op jit(solution)/shard_map/all_gather | solution.py:33
  59.1 20.5 %all_to_all.10 = bf16[4,24,7168]{2,1,0:T(8,128)(2,1)S(1)} all-to-all(bf16[4,24,7168]{2,1,0:T(8,128)(2,1)S(1)} %copy.44), channel_id=1, replica_groups=mesh['ep'=4,'etp'=8] {'ep'}, dimensions={0} | all-to-all | bytes 2752512 | tf_op jit(solution)/shard_map/all_to_all | solution.py:34
  79.6 0.7 fusion.4
  80.3 1.3 copy-done.2
  81.6 0.7 fusion.9
  82.5 2.8 %convolution_convert_fusion.1 = bf16[96,7168]{1,0:T(8,128)(2,1)S(1)} fusion(bf16[96,256]{1,0:T(8,128)(2,1)S(1)} %reshape.58, bf16[1,256,7168]{2,1,0:T(8,128)(2,1)} %param.11), kind=kOutput, calls=%fused_computation.1 | convolution fusion | flops 353009664 | bytes 5095424 | tf_op jit(solution)/shard_map/dot_general | solution.py:42
  85.3 43.2 %fusion = bf16[16,7168]{1,0:T(8,128)(2,1)S(1)} fusion(bf16[96,7168]{1,0:T(8,128)(2,1)S(1)} %convolution_convert_fusion.1), kind=kCustom, calls=%all-reduce-scatter | all-reduce-scatter fusion | flops 917505 | bytes 1606144
  128.5 1.5 collective-permute-start
  130.1 0.1 slice.9
  130.1 4.1 %collective-permute-start.1 = (bf16[12,7168]{1,0:T(8,128)(2,1)S(1)}, bf16[12,7168]{1,0:T(8,128)(2,1)S(1)}, u32[]{:S(2)}, u32[]{:S(2)}) collective-permute-start(bf16[12,7168]{1,0:T(8,128)(2,1)S(1)} %slice.9), channel_id=1, source_target_pairs={{0,2},{1,3},{2,4},{3,5},{4,6},{5,7},{8,10},{9,11},{10,12},{11,13},... | collective-permute-start | bytes 516104
  134.2 0.6 dynamic-slice.4
  135.4 2.3 %collective-permute-done.1 = bf16[12,7168]{1,0:T(8,128)(2,1)S(1)} collective-permute-done((bf16[12,7168]{1,0:T(8,128)(2,1)S(1)}, bf16[12,7168]{1,0:T(8,128)(2,1)S(1)}, u32[]{:S(2)}, u32[]{:S(2)}) %collective-permute-start.1) | collective-permute-done | bytes 172064
  137.7 1.2 concatenate
  138.9 0.1 constant_dynamic-slice_fusion
  139.0 0.1 reshape.59
  139.1 8.0 %all_to_all.11 = bf16[4,3,7168]{2,1,0:T(4,128)(2,1)S(1)} all-to-all(bf16[4,3,7168]{2,1,0:T(4,128)(2,1)S(1)} %reshape.59), channel_id=1, replica_groups=mesh['ep'=4,'etp'=8] {'ep'}, dimensions={0} | all-to-all | bytes 344064 | tf_op jit(solution)/shard_map/all_to_all | solution.py:48
  147.1 0.2 reshape.60
  147.3 2.9 %convolution_convert_fusion = bf16[128,7168]{1,0:T(8,128)(2,1)} fusion(f32[128,12]{0,1:T(8,128)S(1)} %get-tuple-element.6, bf16[12,7168]{1,0:T(8,128)(2,1)S(1)} %reshape.60), kind=kOutput, calls=%fused_computation | convolution fusion | flops 133038080 | bytes 2013184 | tf_op jit(solution)/shard_map/dot_general | solution.py:50
  (17 shorter events, 0.2 us)
Async XLA Ops:
  6.5 4.4 %copy-start = (bf16[128,7168]{1,0:T(8,128)(2,1)S(1)}, bf16[128,7168]{1,0:T(8,128)(2,1)}, u32[]{:S(2)}) copy-start(bf16[128,7168]{1,0:T(8,128)(2,1)} %param.6) | copy-start | bytes 5505028
  6.5 50.7 %all-gather.2.cloned.1.call-start = ((), (), s32[]{:S(2)}) async-start(), calls=%async_computation.2 | async-start | bytes 1548288 | tf_op jit(solution)/shard_map/all_gather | solution.py:33
  57.2 22.4 %copy-start.1 = (bf16[1,7168,256]{2,1,0:T(8,128)(2,1)S(1)}, bf16[1,7168,256]{2,1,0:T(8,128)(2,1)}, u32[]{:S(2)}) copy-start(bf16[1,7168,256]{2,1,0:T(8,128)(2,1)} %param.9) | copy-start | bytes 11010052
  79.6 2.0 %copy-start.2 = (bf16[1,7168,256]{2,1,0:T(8,128)(2,1)S(1)}, bf16[1,7168,256]{2,1,0:T(8,128)(2,1)}, u32[]{:S(2)}) copy-start(bf16[1,7168,256]{2,1,0:T(8,128)(2,1)} %param.10) | copy-start | bytes 11010052
  85.2 48.9 %copy-start.3 = (u32[32]{0:T(128)S(1)}, u32[32]{0:T(128)}, u32[]{:S(2)}) copy-start(u32[32]{0:T(128)} %constant.26) | copy-start | bytes 388
  128.5 9.2 %collective-permute-start = (bf16[16,7168]{1,0:T(8,128)(2,1)S(1)}, bf16[16,7168]{1,0:T(8,128)(2,1)S(1)}, u32[]{:S(2)}, u32[]{:S(2)}) collective-permute-start(bf16[16,7168]{1,0:T(8,128)(2,1)S(1)} %fusion), channel_id=1, source_target_pairs={{0,1},{1,2},{2,3},{3,4},{4,5},{5,6},{6,7},{8,9},{9,10},{10,11},{11... | collective-permute-start | bytes 688136
  130.1 7.6 %collective-permute-start.1 = (bf16[12,7168]{1,0:T(8,128)(2,1)S(1)}, bf16[12,7168]{1,0:T(8,128)(2,1)S(1)}, u32[]{:S(2)}, u32[]{:S(2)}) collective-permute-start(bf16[12,7168]{1,0:T(8,128)(2,1)S(1)} %slice.9), channel_id=1, source_target_pairs={{0,2},{1,3},{2,4},{3,5},{4,6},{5,7},{8,10},{9,11},{10,12},{11,13},... | collective-permute-start | bytes 516104
Sparse Core Ops, SparseCore 0:
  12.3 44.8 all-gather.1
where the time goes:
time: 157 us
  blocking collectives  71.8 us (46%)
  waiting for transfers between devices  47.3 us (30%)
  between operations  14.2 us (9%)
  local copies, waits for them, and re-layouts  7.82 us (5%)
  matrix products  7.42 us (5%)
  starting transfers between devices  5.6 us (4%)
  other arithmetic  2.87 us (2%)
    all_gather x1, waiting for transfers between devices, body(): gathered = lax.all_gather(bucket, 'etp', axis=1, tiled=True)  45 us
    unnamed x1, blocking collectives  43.2 us
    all_to_all x1, blocking collectives, body(): lax.all_to_all(gathered, 'ep', split_axis=0, concat_axis=0, tiled=True)  20.5 us
    all_to_all x1, blocking collectives, body(): lax.all_to_all(local_out, 'ep', split_axis=0, concat_axis=0, tiled=True)  8.03 us
    unnamed x2, starting transfers between devices  5.6 us
    unnamed x13, local copies, waits for them, and re-layouts  4.14 us
  transfers between devices with their start and end apart: 3, of which 2 were waited for; matrix products, arithmetic and copies ran while one was open for 0% of the time, Pallas kernels for 0%

commit v1 on v0

--- a/solution.py
+++ b/solution.py
@@ -4,6 +4,19 @@
 from jax.sharding import PartitionSpec as P
 
 CAP = 3
+
+
+def ring_gather(array, axis, dim):
+    ways = lax.axis_size(axis)
+    up = [(d, (d + 1) % ways) for d in range(ways)]
+    down = [(d, (d - 1) % ways) for d in range(ways)]
+    earlier, later = ([array], [array])
+    for _ in range(ways // 2):
+        earlier.append(lax.ppermute(earlier[-1], axis, up))
+    for _ in range((ways - 1) // 2):
+        later.append(lax.ppermute(later[-1], axis, down))
+    line = jnp.concatenate([*earlier[::-1], *later[1:]], axis=dim)
+    return jnp.roll(line, (lax.axis_index(axis) - ways // 2) * array.shape[dim], axis=dim)
 
 
 def body(tokens, expert_ids, gate_q, w_gate, w_up, w_down):
@@ -30,7 +43,7 @@
         "tc,td->cd", placing.astype(jnp.bfloat16), tokens, preferred_element_type=jnp.float32
     )
     bucket = bucket.astype(jnp.bfloat16).reshape(groups, capacity, width)
-    gathered = lax.all_gather(bucket, "etp", axis=1, tiled=True)
+    gathered = ring_gather(bucket, "etp", 1)
     arrived = lax.all_to_all(gathered, "ep", split_axis=0, concat_axis=0, tiled=True)
     gate = jnp.dot(arrived, w_gate[0], preferred_element_type=jnp.float32)
     upper = jnp.dot(arrived, w_up[0], preferred_element_type=jnp.float32)

time: 157 us -> 201 us (1.28)
  the two profiles are of different devices: /device:TPU:0 before, /device:TPU:26 now
where the time goes in v1:
time: 201 us; the launch traced here: 198 us
  blocking collectives  71.1 us (35%)
  local copies, waits for them, and re-layouts  62.2 us (31%)
  waiting for transfers between devices  44.7 us (22%)
  starting transfers between devices  8.71 us (4%)
  matrix products  7.43 us (4%)
  other arithmetic  2.87 us (1%)
    concatenate x1, local copies, waits for them, and re-layouts, ring_gather(): jnp.roll(line, (lax.axis_index(axis) - ways // 2) * array.shape[dim], axi...  55.1 us
    unnamed x1, blocking collectives  42.5 us
    ppermute x4, waiting for transfers between devices, ring_gather(): earlier.append(lax.ppermute(earlier[-1], axis, up))  36.9 us
    all_to_all x1, blocking collectives, body(): lax.all_to_all(gathered, 'ep', split_axis=0, concat_axis=0, tiled=True)  20.5 us
    all_to_all x1, blocking collectives, body(): lax.all_to_all(local_out, 'ep', split_axis=0, concat_axis=0, tiled=True)  8.03 us
    unnamed x2, waiting for transfers between devices  7.88 us
    ppermute x3, starting transfers between devices, ring_gather(): later.append(lax.ppermute(later[-1], axis, down))  6.06 us
    unnamed x13, local copies, waits for them, and re-layouts  4.14 us
  transfers between devices with their start and end apart: 9, of which 5 were waited for; matrix products, arithmetic and copies ran while one was open for 0% of the time, Pallas kernels for 0%

profile of v1, /device:TPU:26, one launch (start us, length us, event | category | flops | bytes accessed | tf_op | source)
XLA Modules:
  0.0 197.9 jit_solution(9229403574446773840)
XLA Ops:
  0.0 0.9 copy.36
  1.1 1.1 reduce-window.6
  2.3 0.2 slice_reduce_fusion
  2.5 0.2 reduce-window.9
  2.9 0.7 add_select_fusion
  3.6 0.7 convert_multiply_fusion
  4.4 0.3 convolution_convert_fusion.2
  4.7 0.1 reshape.56
  4.9 2.0 %collective-permute-start.4 = (bf16[4,3,7168]{2,1,0:T(4,128)(2,1)S(1)}, bf16[4,3,7168]{2,1,0:T(4,128)(2,1)S(1)}, u32[]{:S(2)}, u32[]{:S(2)}) collective-permute-start(bf16[4,3,7168]{2,1,0:T(4,128)(2,1)S(1)} %reshape.56), channel_id=1, source_target_pairs={{0,7},{1,0},{2,1},{3,2},{4,3},{5,4},{6,5},{7,6},{8,15},{9,8},{10,9... | collective-permute-start | bytes 516104 | tf_op jit(solution)/shard_map/ppermute | solution.py:17
  6.9 10.2 %collective-permute-done = bf16[4,3,7168]{2,1,0:T(4,128)(2,1)S(1)} collective-permute-done((bf16[4,3,7168]{2,1,0:T(4,128)(2,1)S(1)}, bf16[4,3,7168]{2,1,0:T(4,128)(2,1)S(1)}, u32[]{:S(2)}, u32[]{:S(2)}) %collective-permute-start) | collective-permute-done | bytes 172064 | tf_op jit(solution)/shard_map/ppermute | solution.py:15
  17.2 2.0 %collective-permute-start.5 = (bf16[4,3,7168]{2,1,0:T(4,128)(2,1)S(1)}, bf16[4,3,7168]{2,1,0:T(4,128)(2,1)S(1)}, u32[]{:S(2)}, u32[]{:S(2)}) collective-permute-start(bf16[4,3,7168]{2,1,0:T(4,128)(2,1)S(1)} %collective-permute-done.4), channel_id=1, source_target_pairs={{0,7},{1,0},{2,1},{3,2},{4,3},{5,4},{6,5},{7,6},{8,15},{9,8},{10,9... | collective-permute-start | bytes 516104 | tf_op jit(solution)/shard_map/ppermute | solution.py:17
  19.2 9.4 %collective-permute-done.1 = bf16[4,3,7168]{2,1,0:T(4,128)(2,1)S(1)} collective-permute-done((bf16[4,3,7168]{2,1,0:T(4,128)(2,1)S(1)}, bf16[4,3,7168]{2,1,0:T(4,128)(2,1)S(1)}, u32[]{:S(2)}, u32[]{:S(2)}) %collective-permute-start.1) | collective-permute-done | bytes 172064 | tf_op jit(solution)/shard_map/ppermute | solution.py:15
  28.6 2.0 %collective-permute-start.6 = (bf16[4,3,7168]{2,1,0:T(4,128)(2,1)S(1)}, bf16[4,3,7168]{2,1,0:T(4,128)(2,1)S(1)}, u32[]{:S(2)}, u32[]{:S(2)}) collective-permute-start(bf16[4,3,7168]{2,1,0:T(4,128)(2,1)S(1)} %collective-permute-done.5), channel_id=1, source_target_pairs={{0,7},{1,0},{2,1},{3,2},{4,3},{5,4},{6,5},{7,6},{8,15},{9,8},{10,9... | collective-permute-start | bytes 516104 | tf_op jit(solution)/shard_map/ppermute | solution.py:17
  30.6 11.1 %collective-permute-done.2 = bf16[4,3,7168]{2,1,0:T(4,128)(2,1)S(1)} collective-permute-done((bf16[4,3,7168]{2,1,0:T(4,128)(2,1)S(1)}, bf16[4,3,7168]{2,1,0:T(4,128)(2,1)S(1)}, u32[]{:S(2)}, u32[]{:S(2)}) %collective-permute-start.2) | collective-permute-done | bytes 172064 | tf_op jit(solution)/shard_map/ppermute | solution.py:15
  41.7 6.1 %collective-permute-done.3 = bf16[4,3,7168]{2,1,0:T(4,128)(2,1)} collective-permute-done((bf16[4,3,7168]{2,1,0:T(4,128)(2,1)S(1)}, bf16[4,3,7168]{2,1,0:T(4,128)(2,1)}, u32[]{:S(2)}, u32[]{:S(2)}) %collective-permute-start.3) | collective-permute-done | bytes 172064 | tf_op jit(solution)/shard_map/ppermute | solution.py:15
  47.8 55.1 %concatenate.6 = bf16[4,48,7168]{2,1,0:T(8,128)(2,1)} concatenate(bf16[4,3,7168]{2,1,0:T(4,128)(2,1)} %collective-permute-done.3, bf16[4,3,7168]{2,1,0:T(4,128)(2,1)S(1)} %collective-permute-done.2, bf16[4,3,7168]{2,1,0:T(4,128)(2,1)S(1)} %collective-permute-done.1, bf16[4,3,7168]{2,1,0:T(4,128)(2,1)S(1)} %collective-permute-done, bf16[4,3,7168]{2,1,0:T(4,128)(2,1)S(1)} %reshape.56, ...), dimensions={1} | concatenate | bytes 5505024 | tf_op jit(solution)/shard_map/jit(_roll_dynamic)/concatenate | solution.py:19
  102.9 2.0 %constant_dynamic-slice_fusion.1 = bf16[4,24,7168]{2,1,0:T(8,128)(2,1)S(1)} fusion(bf16[4,48,7168]{2,1,0:T(8,128)(2,1)} %concatenate.6, s32[]{:T(128)S(6)} %select_n.23), kind=kLoop, calls=%fused_computation.25 | loop fusion | bytes 2752516 | tf_op jit(solution)/shard_map/jit(_roll_dynamic)/dynamic_slice | solution.py:19
  104.9 20.5 %all_to_all.10 = bf16[4,24,7168]{2,1,0:T(8,128)(2,1)S(1)} all-to-all(bf16[4,24,7168]{2,1,0:T(8,128)(2,1)S(1)} %constant_dynamic-slice_fusion.1), channel_id=1, replica_groups=mesh['ep'=4,'etp'=8] {'ep'}, dimensions={0} | all-to-all | bytes 2752512 | tf_op jit(solution)/shard_map/all_to_all | solution.py:47
  125.5 0.7 fusion.4
  126.2 1.3 copy-done.2
  127.5 0.7 multiply_convert_fusion
  128.4 2.8 %convolution_convert_fusion.1 = bf16[96,7168]{1,0:T(8,128)(2,1)S(1)} fusion(bf16[96,256]{1,0:T(8,128)(2,1)S(1)} %reshape.58, bf16[1,256,7168]{2,1,0:T(8,128)(2,1)} %param.11), kind=kOutput, calls=%fused_computation.1 | convolution fusion | flops 353009664 | bytes 5095424 | tf_op jit(solution)/shard_map/dot_general | solution.py:55
  131.1 42.5 %fusion = bf16[16,7168]{1,0:T(8,128)(2,1)S(1)} fusion(bf16[96,7168]{1,0:T(8,128)(2,1)S(1)} %convolution_convert_fusion.1), kind=kCustom, calls=%all-reduce-scatter | all-reduce-scatter fusion | flops 917505 | bytes 1606144
  173.6 1.3 collective-permute-start.7
  175.0 1.3 collective-permute-start.8
  176.3 0.6 dynamic-slice.4
  177.5 7.9 %collective-permute-done.8 = bf16[12,7168]{1,0:T(8,128)(2,1)S(1)} collective-permute-done((bf16[12,7168]{1,0:T(8,128)(2,1)S(1)}, bf16[12,7168]{1,0:T(8,128)(2,1)S(1)}, u32[]{:S(2)}, u32[]{:S(2)}) %collective-permute-start.8) | collective-permute-done | bytes 172064
  185.4 1.2 concatenate.7
  186.7 0.1 reshape.59
  186.8 8.0 %all_to_all.11 = bf16[4,3,7168]{2,1,0:T(4,128)(2,1)S(1)} all-to-all(bf16[4,3,7168]{2,1,0:T(4,128)(2,1)S(1)} %reshape.59), channel_id=1, replica_groups=mesh['ep'=4,'etp'=8] {'ep'}, dimensions={0} | all-to-all | bytes 344064 | tf_op jit(solution)/shard_map/all_to_all | solution.py:61
  194.9 0.2 reshape.60
  195.0 2.9 %convolution_convert_fusion = bf16[128,7168]{1,0:T(8,128)(2,1)} fusion(f32[128,12]{0,1:T(8,128)S(1)} %get-tuple-element.6, bf16[12,7168]{1,0:T(8,128)(2,1)S(1)} %reshape.60), kind=kOutput, calls=%fused_computation | convolution fusion | flops 133038080 | bytes 2013184 | tf_op jit(solution)/shard_map/dot_general | solution.py:63
  (28 shorter events, 0.8 us)
Async XLA Ops:
  0.0 4.4 %copy-start = (bf16[128,7168]{1,0:T(8,128)(2,1)S(1)}, bf16[128,7168]{1,0:T(8,128)(2,1)}, u32[]{:S(2)}) copy-start(bf16[128,7168]{1,0:T(8,128)(2,1)} %param.6) | copy-start | bytes 5505028
  4.8 12.3 %collective-permute-start = (bf16[4,3,7168]{2,1,0:T(4,128)(2,1)S(1)}, bf16[4,3,7168]{2,1,0:T(4,128)(2,1)S(1)}, u32[]{:S(2)}, u32[]{:S(2)}) collective-permute-start(bf16[4,3,7168]{2,1,0:T(4,128)(2,1)S(1)} %reshape.56), channel_id=1, source_target_pairs={{0,1},{1,2},{2,3},{3,4},{4,5},{5,6},{6,7},{7,0},{8,9},{9,10},{10,1... | collective-permute-start | bytes 516104 | tf_op jit(solution)/shard_map/ppermute | solution.py:15
  4.9 12.3 %collective-permute-start.4 = (bf16[4,3,7168]{2,1,0:T(4,128)(2,1)S(1)}, bf16[4,3,7168]{2,1,0:T(4,128)(2,1)S(1)}, u32[]{:S(2)}, u32[]{:S(2)}) collective-permute-start(bf16[4,3,7168]{2,1,0:T(4,128)(2,1)S(1)} %reshape.56), channel_id=1, source_target_pairs={{0,7},{1,0},{2,1},{3,2},{4,3},{5,4},{6,5},{7,6},{8,15},{9,8},{10,9... | collective-permute-start | bytes 516104 | tf_op jit(solution)/shard_map/ppermute | solution.py:17
  17.2 11.4 %collective-permute-start.1 = (bf16[4,3,7168]{2,1,0:T(4,128)(2,1)S(1)}, bf16[4,3,7168]{2,1,0:T(4,128)(2,1)S(1)}, u32[]{:S(2)}, u32[]{:S(2)}) collective-permute-start(bf16[4,3,7168]{2,1,0:T(4,128)(2,1)S(1)} %collective-permute-done), channel_id=1, source_target_pairs={{0,1},{1,2},{2,3},{3,4},{4,5},{5,6},{6,7},{7,0},{8,9},{9,10},{10,1... | collective-permute-start | bytes 516104 | tf_op jit(solution)/shard_map/ppermute | solution.py:15
  17.2 11.4 %collective-permute-start.5 = (bf16[4,3,7168]{2,1,0:T(4,128)(2,1)S(1)}, bf16[4,3,7168]{2,1,0:T(4,128)(2,1)S(1)}, u32[]{:S(2)}, u32[]{:S(2)}) collective-permute-start(bf16[4,3,7168]{2,1,0:T(4,128)(2,1)S(1)} %collective-permute-done.4), channel_id=1, source_target_pairs={{0,7},{1,0},{2,1},{3,2},{4,3},{5,4},{6,5},{7,6},{8,15},{9,8},{10,9... | collective-permute-start | bytes 516104 | tf_op jit(solution)/shard_map/ppermute | solution.py:17
  28.6 13.2 %collective-permute-start.2 = (bf16[4,3,7168]{2,1,0:T(4,128)(2,1)S(1)}, bf16[4,3,7168]{2,1,0:T(4,128)(2,1)S(1)}, u32[]{:S(2)}, u32[]{:S(2)}) collective-permute-start(bf16[4,3,7168]{2,1,0:T(4,128)(2,1)S(1)} %collective-permute-done.1), channel_id=1, source_target_pairs={{0,1},{1,2},{2,3},{3,4},{4,5},{5,6},{6,7},{7,0},{8,9},{9,10},{10,1... | collective-permute-start | bytes 516104 | tf_op jit(solution)/shard_map/ppermute | solution.py:15
  28.6 13.2 %collective-permute-start.6 = (bf16[4,3,7168]{2,1,0:T(4,128)(2,1)S(1)}, bf16[4,3,7168]{2,1,0:T(4,128)(2,1)S(1)}, u32[]{:S(2)}, u32[]{:S(2)}) collective-permute-start(bf16[4,3,7168]{2,1,0:T(4,128)(2,1)S(1)} %collective-permute-done.5), channel_id=1, source_target_pairs={{0,7},{1,0},{2,1},{3,2},{4,3},{5,4},{6,5},{7,6},{8,15},{9,8},{10,9... | collective-permute-start | bytes 516104 | tf_op jit(solution)/shard_map/ppermute | solution.py:17
  41.7 6.1 %collective-permute-start.3 = (bf16[4,3,7168]{2,1,0:T(4,128)(2,1)S(1)}, bf16[4,3,7168]{2,1,0:T(4,128)(2,1)}, u32[]{:S(2)}, u32[]{:S(2)}) collective-permute-start(bf16[4,3,7168]{2,1,0:T(4,128)(2,1)S(1)} %collective-permute-done.2), channel_id=1, source_target_pairs={{0,1},{1,2},{2,3},{3,4},{4,5},{5,6},{6,7},{7,0},{8,9},{9,10},{10,1... | collective-permute-start | bytes 516104 | tf_op jit(solution)/shard_map/ppermute | solution.py:15
  102.9 22.6 %copy-start.1 = (bf16[1,7168,256]{2,1,0:T(8,128)(2,1)S(1)}, bf16[1,7168,256]{2,1,0:T(8,128)(2,1)}, u32[]{:S(2)}) copy-start(bf16[1,7168,256]{2,1,0:T(8,128)(2,1)} %param.9) | copy-start | bytes 11010052
  125.5 2.0 %copy-start.2 = (bf16[1,7168,256]{2,1,0:T(8,128)(2,1)S(1)}, bf16[1,7168,256]{2,1,0:T(8,128)(2,1)}, u32[]{:S(2)}) copy-start(bf16[1,7168,256]{2,1,0:T(8,128)(2,1)} %param.10) | copy-start | bytes 11010052
  131.1 45.2 %copy-start.3 = (u32[32]{0:T(128)S(1)}, u32[32]{0:T(128)}, u32[]{:S(2)}) copy-start(u32[32]{0:T(128)} %constant.52) | copy-start | bytes 388
  173.6 11.8 %collective-permute-start.7 = (bf16[16,7168]{1,0:T(8,128)(2,1)S(1)}, bf16[16,7168]{1,0:T(8,128)(2,1)S(1)}, u32[]{:S(2)}, u32[]{:S(2)}) collective-permute-start(bf16[16,7168]{1,0:T(8,128)(2,1)S(1)} %fusion), channel_id=1, source_target_pairs={{0,1},{1,2},{2,3},{3,4},{4,5},{5,6},{6,7},{8,9},{9,10},{10,11},{11... | collective-permute-start | bytes 688136
  175.0 10.4 %collective-permute-start.8 = (bf16[12,7168]{1,0:T(8,128)(2,1)S(1)}, bf16[12,7168]{1,0:T(8,128)(2,1)S(1)}, u32[]{:S(2)}, u32[]{:S(2)}) collective-permute-start(bf16[12,7168]{1,0:T(8,128)(2,1)S(1)} %slice.9), channel_id=1, source_target_pairs={{0,2},{1,3},{2,4},{3,5},{4,6},{5,7},{8,10},{9,11},{10,12},{11,13},... | collective-permute-start | bytes 516104
